TPU v7x, 32 devices: a whole 2x2x4 slice. The times are simulated.
32 devices in a mesh: fsdp: 16 (over z, x, core), tp: 2 (over y).
Axes of the slice: x: 2, y: 2, z: 4, core: 2. Of those that a mesh axis runs over, the one named last changes fastest.
Arguments:
- block_input: bfloat16 [3072, 2304], P(('fsdp', 'tp')), may hold values from -6 to 6
- lengths: int32 [16, 9], P('fsdp'), may hold values from 1 to 96, 192 in all within a row
- attention_norm_gain: bfloat16 [2304], P('fsdp'), may hold values from 0.25 to 1.75
- attention_post_gain: bfloat16 [2304], P('fsdp'), may hold values from 0.25 to 1.75
- feedforward_norm_gain: bfloat16 [2304], P('fsdp'), may hold values from 0.25 to 1.75
- feedforward_post_gain: bfloat16 [2304], P('fsdp'), may hold values from 0.25 to 1.75
- query_weight: bfloat16 [2304, 2048], P('fsdp', 'tp'), may hold values from -0.125 to 0.125
- key_weight: bfloat16 [2304, 1024], P('fsdp', 'tp'), may hold values from -0.125 to 0.125
- value_weight: bfloat16 [2304, 1024], P('fsdp', 'tp'), may hold values from -0.125 to 0.125
- output_weight: bfloat16 [2304, 2048], P('fsdp', 'tp'), may hold values from -0.125 to 0.125
- gate_weight: bfloat16 [2304, 9216], P('fsdp', 'tp'), may hold values from -0.125 to 0.125
- up_weight: bfloat16 [2304, 9216], P('fsdp', 'tp'), may hold values from -0.125 to 0.125
- down_weight: bfloat16 [2304, 9216], P('fsdp', 'tp'), may hold values from -0.0625 to 0.0625
- output_cotangent: bfloat16 [3072, 2304], P(('fsdp', 'tp')), may hold values from -6 to 6
Outputs:
- block_output: bfloat16 [3072, 2304], P(('fsdp', 'tp'))
- input_gradient: float32 [3072, 2304], P(('fsdp', 'tp'))
- attention_norm_gain_gradient: float32 [2304], P('fsdp')
- attention_post_gain_gradient: float32 [2304], P('fsdp')
- feedforward_norm_gain_gradient: float32 [2304], P('fsdp')
- feedforward_post_gain_gradient: float32 [2304], P('fsdp')
- query_weight_gradient: float32 [2304, 2048], P('fsdp', 'tp')
- key_weight_gradient: float32 [2304, 1024], P('fsdp', 'tp')
- value_weight_gradient: float32 [2304, 1024], P('fsdp', 'tp')
- output_weight_gradient: float32 [2304, 2048], P('fsdp', 'tp')
- gate_weight_gradient: float32 [2304, 9216], P('fsdp', 'tp')
- up_weight_gradient: float32 [2304, 9216], P('fsdp', 'tp')
- down_weight_gradient: float32 [2304, 9216], P('fsdp', 'tp')
Inputs may be any that keep to these rules, and one draw needn't show every extreme that they name: `lengths`: row g gives the length of group g's prompt (column 0) and of its 8 continuations; each row sums to 192, and its largest entry is 96.
All inputs are finite; a program needn't handle non-finite values.
Results may differ from a plain program's by a relative error of at most 0.017.
Values may be sent and summed in bfloat16 or wider, within the bound.
A program may use at most 512 MiB of HBM per device.

v0:
```python
import math
import jax
import jax.numpy as jnp
from jax import lax
from jax.sharding import PartitionSpec as P

HEAD_SIZE = 256
EPSILON = 1e-06
SOFTCAP = 50.0
NEGATIVE = -1e30


def contract_last(left_rows, right_rows):
    return lax.dot_general(
        left_rows, right_rows, (((1,), (1,)), ((), ())), preferred_element_type=jnp.float32
    )


def contract_first(left_rows, right_rows):
    return lax.dot_general(
        left_rows, right_rows, (((0,), (0,)), ((), ())), preferred_element_type=jnp.float32
    )


def normalize_parts(value_rows):
    inverse = lax.rsqrt(jnp.mean(value_rows * value_rows, axis=-1, keepdims=True) + EPSILON)
    return (value_rows * inverse, inverse)


def norm_backward(unit_rows, inverse, norm_gain, upstream):
    scaled = upstream * norm_gain
    return inverse * (scaled - unit_rows * jnp.mean(scaled * unit_rows, axis=-1, keepdims=True))


def layout(lengths_row, grouped_rows):
    segment_ends = jnp.cumsum(lengths_row)
    segment_starts = segment_ends - lengths_row
    row_index = jnp.arange(grouped_rows, dtype=jnp.int32)
    segment = jnp.sum((row_index[:, None] >= segment_ends[None, :]).astype(jnp.int32), axis=1)
    onehot = segment[:, None] == jnp.arange(lengths_row.shape[0], dtype=jnp.int32)[None, :]
    segment_begin = jnp.sum(jnp.where(onehot, segment_starts[None, :], 0), axis=1)
    prompt_shift = jnp.where(segment > 0, lengths_row[0], 0)
    return (segment, row_index - segment_begin + prompt_shift)


def rotary_tables(position):
    frequency = jnp.exp(
        jnp.arange(HEAD_SIZE // 2, dtype=jnp.float32) * (-2.0 * math.log(10000.0) / HEAD_SIZE)
    )
    angles = position.astype(jnp.float32)[:, None] * frequency[None, :]
    return (jnp.cos(angles), jnp.sin(angles))


def apply_rotary(value_rows, cosine_lookup, sine_lookup):
    half_width = value_rows.shape[-1] // 2
    first_half = value_rows[..., :half_width]
    second_half = value_rows[..., half_width:]
    cosine_part = cosine_lookup[:, None, :]
    sine_part = sine_lookup[:, None, :]
    return jnp.concatenate(
        [
            first_half * cosine_part - second_half * sine_part,
            second_half * cosine_part + first_half * sine_part,
        ],
        axis=-1,
    )


def unrotate(value_rows, cosine_lookup, sine_lookup):
    half_width = value_rows.shape[-1] // 2
    first_half = value_rows[..., :half_width]
    second_half = value_rows[..., half_width:]
    cosine_part = cosine_lookup[:, None, :]
    sine_part = sine_lookup[:, None, :]
    return jnp.concatenate(
        [
            first_half * cosine_part + second_half * sine_part,
            second_half * cosine_part - first_half * sine_part,
        ],
        axis=-1,
    )


def visible(segment):
    row_index = jnp.arange(segment.shape[0], dtype=jnp.int32)
    same_segment = (segment[:, None] == segment[None, :]) & (
        row_index[None, :] <= row_index[:, None]
    )
    from_prompt = (segment[None, :] == 0) & (segment[:, None] > 0)
    return same_segment | from_prompt


def masked_scores(rotated_query, rotated_key, visible_mask):
    raw_scores = jnp.einsum(
        "qgrd,kgd->grqk", rotated_query, rotated_key, preferred_element_type=jnp.float32
    )
    tanh_value = jnp.tanh(raw_scores * HEAD_SIZE ** (-0.5) / SOFTCAP)
    return (jnp.where(visible_mask[None, None], SOFTCAP * tanh_value, NEGATIVE), tanh_value)


def gelu_product(gate_value, up_value):
    return jax.nn.gelu(gate_value, approximate=True) * up_value


def shards(
    block_input,
    lengths,
    attention_norm_gain,
    attention_post_gain,
    feedforward_norm_gain,
    feedforward_post_gain,
    query_weight,
    key_weight,
    value_weight,
    output_weight,
    gate_weight,
    up_weight,
    down_weight,
    output_cotangent,
):
    query_full, key_full, value_full, output_full, gain_one, gain_two = (
        lax.all_gather(query_weight, "fsdp", axis=0, tiled=True),
        lax.all_gather(key_weight, "fsdp", axis=0, tiled=True),
        lax.all_gather(value_weight, "fsdp", axis=0, tiled=True),
        lax.all_gather(output_weight, "fsdp", axis=0, tiled=True),
        lax.all_gather(attention_norm_gain, "fsdp", axis=0, tiled=True),
        lax.all_gather(attention_post_gain, "fsdp", axis=0, tiled=True),
    )
    gate_full, up_full, down_full, gain_three, gain_four = (
        lax.all_gather(gate_weight, "fsdp", axis=0, tiled=True),
        lax.all_gather(up_weight, "fsdp", axis=0, tiled=True),
        lax.all_gather(down_weight, "fsdp", axis=0, tiled=True),
        lax.all_gather(feedforward_norm_gain, "fsdp", axis=0, tiled=True),
        lax.all_gather(feedforward_post_gain, "fsdp", axis=0, tiled=True),
    )
    gain_one = gain_one.astype(jnp.float32)
    gain_two = gain_two.astype(jnp.float32)
    gain_three = gain_three.astype(jnp.float32)
    gain_four = gain_four.astype(jnp.float32)
    rows_local = block_input.shape[0]
    grouped_rows = rows_local * lax.axis_size("tp")
    segment, position = layout(lengths[0], grouped_rows)
    cosine_lookup, sine_lookup = rotary_tables(position)
    visible_mask = visible(segment)
    residual = block_input.astype(jnp.float32)
    unit_one, inverse_one = normalize_parts(residual)
    normed_local = (unit_one * gain_one).astype(jnp.bfloat16)
    normed = lax.all_gather(normed_local, "tp", axis=0, tiled=True)
    query_raw = jnp.dot(normed, query_full, preferred_element_type=jnp.float32)
    key_raw = jnp.dot(normed, key_full, preferred_element_type=jnp.float32)
    value_raw = jnp.dot(normed, value_full, preferred_element_type=jnp.float32)
    heads_local = query_raw.shape[1] // HEAD_SIZE
    kv_local = key_raw.shape[1] // HEAD_SIZE
    repeat_heads = heads_local // kv_local
    rotated_query = apply_rotary(
        query_raw.reshape(grouped_rows, heads_local, HEAD_SIZE), cosine_lookup, sine_lookup
    ).astype(jnp.bfloat16)
    rotated_query = rotated_query.reshape(grouped_rows, kv_local, repeat_heads, HEAD_SIZE)
    rotated_key = apply_rotary(
        key_raw.reshape(grouped_rows, kv_local, HEAD_SIZE), cosine_lookup, sine_lookup
    ).astype(jnp.bfloat16)
    value_reduced = value_raw.astype(jnp.bfloat16).reshape(grouped_rows, kv_local, HEAD_SIZE)
    capped, tanh_value = masked_scores(rotated_query, rotated_key, visible_mask)
    row_peak = jnp.max(capped, axis=-1, keepdims=True)
    log_total = row_peak + jnp.log(jnp.sum(jnp.exp(capped - row_peak), axis=-1, keepdims=True))
    softmax_probs = jnp.exp(capped - log_total)
    mixed_heads = jnp.einsum(
        "grqk,kgd->qgrd",
        softmax_probs.astype(jnp.bfloat16),
        value_reduced,
        preferred_element_type=jnp.float32,
    )
    attended = mixed_heads.reshape(grouped_rows, heads_local * HEAD_SIZE).astype(jnp.bfloat16)
    row_piece = attended
    branch_one = lax.psum_scatter(
        contract_last(row_piece, output_full), "tp", scatter_dimension=0, tiled=True
    )
    unit_two, inverse_two = normalize_parts(branch_one)
    middle = residual + unit_two * gain_two
    unit_three, inverse_three = normalize_parts(middle)
    feed_local = (unit_three * gain_three).astype(jnp.bfloat16)
    feed_input = lax.all_gather(feed_local, "tp", axis=0, tiled=True)
    gate_value = jnp.dot(feed_input, gate_full, preferred_element_type=jnp.float32)
    up_value = jnp.dot(feed_input, up_full, preferred_element_type=jnp.float32)
    hidden = gelu_product(gate_value, up_value).astype(jnp.bfloat16)
    row_piece = hidden
    branch_two = lax.psum_scatter(
        contract_last(row_piece, down_full), "tp", scatter_dimension=0, tiled=True
    )
    unit_four, inverse_four = normalize_parts(branch_two)
    block_output = (middle + unit_four * gain_four).astype(jnp.bfloat16)
    upstream = output_cotangent.astype(jnp.float32)
    gain_four_grad = jnp.sum(upstream * unit_four, axis=0)
    branch_two_grad = norm_backward(unit_four, inverse_four, gain_four, upstream).astype(
        jnp.bfloat16
    )
    held_back = lax.optimization_barrier(
        (
            query_weight,
            key_weight,
            value_weight,
            output_weight,
            gate_weight,
            up_weight,
            down_weight,
            branch_two_grad,
        )
    )
    query_full, key_full, value_full, output_full, gate_full, up_full, down_full = (
        lax.all_gather(held_back[0], "fsdp", axis=0, tiled=True),
        lax.all_gather(held_back[1], "fsdp", axis=0, tiled=True),
        lax.all_gather(held_back[2], "fsdp", axis=0, tiled=True),
        lax.all_gather(held_back[3], "fsdp", axis=0, tiled=True),
        lax.all_gather(held_back[4], "fsdp", axis=0, tiled=True),
        lax.all_gather(held_back[5], "fsdp", axis=0, tiled=True),
        lax.all_gather(held_back[6], "fsdp", axis=0, tiled=True),
    )
    branch_two_grad = held_back[7]
    feed_grad_rows = lax.all_gather(branch_two_grad, "tp", axis=0, tiled=True)
    hidden_grad = jnp.dot(feed_grad_rows, down_full, preferred_element_type=jnp.float32)
    unused_out, pullback = jax.vjp(gelu_product, gate_value, up_value)
    gate_grad, up_grad = pullback(hidden_grad)
    gate_up_grad = jnp.concatenate(
        [gate_grad.astype(jnp.bfloat16), up_grad.astype(jnp.bfloat16)], axis=1
    )
    feed_split = gate_full.shape[1]
    shard_rows = query_weight.shape[0]
    left_rows = feed_input
    feed_weight_grads = lax.psum_scatter(
        jnp.concatenate(
            [contract_first(left_rows, gate_up_grad), contract_first(feed_grad_rows, hidden)],
            axis=1,
        ),
        "fsdp",
        scatter_dimension=0,
        tiled=True,
    )
    row_piece = gate_up_grad
    normed_three_grad = lax.psum_scatter(
        contract_last(row_piece[:, :feed_split], gate_full)
        + contract_last(row_piece[:, feed_split:], up_full),
        "tp",
        scatter_dimension=0,
        tiled=True,
    )
    gain_three_grad = jnp.sum(normed_three_grad * unit_three, axis=0)
    middle_grad = upstream + norm_backward(unit_three, inverse_three, gain_three, normed_three_grad)
    gain_two_grad = jnp.sum(middle_grad * unit_two, axis=0)
    branch_one_grad = norm_backward(unit_two, inverse_two, gain_two, middle_grad).astype(
        jnp.bfloat16
    )
    attention_grad_rows = lax.all_gather(branch_one_grad, "tp", axis=0, tiled=True)
    mixed_grad = jnp.dot(
        attention_grad_rows, output_full, preferred_element_type=jnp.float32
    ).astype(jnp.bfloat16)
    mixed_grad = mixed_grad.reshape(grouped_rows, kv_local, repeat_heads, HEAD_SIZE)
    capped_again, tanh_again = masked_scores(rotated_query, rotated_key, visible_mask)
    probs_again = jnp.exp(capped_again - log_total)
    value_grad = jnp.einsum(
        "grqk,qgrd->kgd",
        probs_again.astype(jnp.bfloat16),
        mixed_grad,
        preferred_element_type=jnp.float32,
    )
    probs_grad = jnp.einsum(
        "qgrd,kgd->grqk", mixed_grad, value_reduced, preferred_element_type=jnp.float32
    )
    score_grad = probs_again * (
        probs_grad - jnp.sum(probs_again * probs_grad, axis=-1, keepdims=True)
    )
    raw_grad = (score_grad * (1.0 - tanh_again * tanh_again) * HEAD_SIZE ** (-0.5)).astype(
        jnp.bfloat16
    )
    query_grad = jnp.einsum(
        "grqk,kgd->qgrd", raw_grad, rotated_key, preferred_element_type=jnp.float32
    )
    key_grad = jnp.einsum(
        "grqk,qgrd->kgd", raw_grad, rotated_query, preferred_element_type=jnp.float32
    )
    query_grad = unrotate(
        query_grad.reshape(grouped_rows, heads_local, HEAD_SIZE), cosine_lookup, sine_lookup
    )
    key_grad = unrotate(key_grad, cosine_lookup, sine_lookup)
    projected_grad = jnp.concatenate(
        [
            query_grad.reshape(grouped_rows, heads_local * HEAD_SIZE).astype(jnp.bfloat16),
            key_grad.reshape(grouped_rows, kv_local * HEAD_SIZE).astype(jnp.bfloat16),
            value_grad.reshape(grouped_rows, kv_local * HEAD_SIZE).astype(jnp.bfloat16),
        ],
        axis=1,
    )
    query_width = query_full.shape[1]
    key_width = key_full.shape[1]
    left_rows = normed
    attention_weight_grads = lax.psum_scatter(
        jnp.concatenate(
            [
                contract_first(left_rows, projected_grad),
                contract_first(attention_grad_rows, attended),
            ],
            axis=1,
        ),
        "fsdp",
        scatter_dimension=0,
        tiled=True,
    )
    row_piece = projected_grad
    total = contract_last(row_piece[:, :query_width], query_full)
    total = total + contract_last(row_piece[:, query_width : query_width + key_width], key_full)
    normed_one_grad = lax.psum_scatter(
        (total + contract_last(row_piece[:, query_width + key_width :], value_full)).astype(
            jnp.bfloat16
        ),
        "tp",
        scatter_dimension=0,
        tiled=True,
    ).astype(jnp.float32)
    gain_one_grad = jnp.sum(normed_one_grad * unit_one, axis=0)
    input_gradient = middle_grad + norm_backward(unit_one, inverse_one, gain_one, normed_one_grad)
    gain_sums = lax.psum(
        (gain_one_grad, gain_two_grad, gain_three_grad, gain_four_grad), ("fsdp", "tp")
    )
    offset = lax.axis_index("fsdp") * shard_rows
    gain_shards = [
        lax.dynamic_slice_in_dim(total_sum, offset, shard_rows) for total_sum in gain_sums
    ]
    value_start = query_width + key_width
    output_start = value_start + key_width
    return (
        block_output,
        input_gradient,
        gain_shards[0],
        gain_shards[1],
        gain_shards[2],
        gain_shards[3],
        attention_weight_grads[:, :query_width],
        attention_weight_grads[:, query_width:value_start],
        attention_weight_grads[:, value_start:output_start],
        attention_weight_grads[:, output_start:],
        feed_weight_grads[:, :feed_split],
        feed_weight_grads[:, feed_split : 2 * feed_split],
        feed_weight_grads[:, 2 * feed_split :],
    )


def solution(mesh):
    placed = (
        P(("fsdp", "tp"), None),
        P("fsdp", None),
        P("fsdp"),
        P("fsdp"),
        P("fsdp"),
        P("fsdp"),
        P("fsdp", "tp"),
        P("fsdp", "tp"),
        P("fsdp", "tp"),
        P("fsdp", "tp"),
        P("fsdp", "tp"),
        P("fsdp", "tp"),
        P("fsdp", "tp"),
        P(("fsdp", "tp"), None),
    )
    return jax.shard_map(
        shards,
        mesh=mesh,
        in_specs=placed,
        out_specs=(
            P(("fsdp", "tp"), None),
            P(("fsdp", "tp"), None),
            P("fsdp"),
            P("fsdp"),
            P("fsdp"),
            P("fsdp"),
            P("fsdp", "tp"),
            P("fsdp", "tp"),
            P("fsdp", "tp"),
            P("fsdp", "tp"),
            P("fsdp", "tp"),
            P("fsdp", "tp"),
            P("fsdp", "tp"),
        ),
        check_vma=False,
    )
```

profile of v0, /device:TPU:0, one launch (start us, length us, event | category | flops | bytes accessed | tf_op | source)
XLA Modules:
  0.0 2708.5 jit_solution(12363852051479386329)
XLA Ops:
  15.4 63.9 %all-reduce.5 = (bf16[2304]{0:T(1024)(128)(2,1)S(1)}, bf16[2304]{0:T(1024)(128)(2,1)S(1)}, bf16[2304]{0:T(1024)(128)(2,1)S(1)}, bf16[2304]{0:T(1024)(128)(2,1)S(1)}) all-reduce(bf16[2304]{0:T(1024)(128)(2,1)S(1)} %dynamic-update-slice, bf16[2304]{0:T(1024)(128)(2,1)S(1)} %dynamic-update-slice.1, ...), channel_id=1, replica_groups=mesh['fsdp'=16,'tp'=2] {'fsdp'}, use_global_device_ids=true, to_apply=%add | all-reduce | flops 9216 | bytes 36864
  83.3 9.0 all_gather.67
  93.0 2.3 fusion.107
  95.6 3.4 all-gather.15.cloned.1.call-done
  101.6 51.6 %all-gather.19.cloned.1.call-done = bf16[2304,1024]{1,0:T(8,128)(2,1)} async-done(((bf16[144,1024]{1,0:T(8,128)(2,1)}), bf16[2304,1024]{1,0:T(8,128)(2,1)}) %all-gather.19.cloned.1.call-update) | async-done | bytes 4718608 | tf_op jit(solution)/shard_map/all_gather | solution.py:122
  153.2 3.4 fusion.108
  159.3 47.7 %all-gather.21.cloned.1.call-done = bf16[2304,1024]{1,0:T(8,128)(2,1)} async-done(((bf16[144,1024]{1,0:T(8,128)(2,1)}), bf16[2304,1024]{1,0:T(8,128)(2,1)}) %all-gather.21.cloned.1.call-update) | async-done | bytes 4718608 | tf_op jit(solution)/shard_map/all_gather | solution.py:125
  207.0 5.2 fusion.109
  214.4 24.9 reduce-scatter.9.cloned.1.call-done
  242.3 12.7 all_gather.74
  255.1 95.7 %all-gather.23.cloned.1.call-done = bf16[2304,4608]{1,0:T(8,128)(2,1)} async-done(((bf16[144,4608]{1,0:T(8,128)(2,1)}), bf16[2304,4608]{1,0:T(8,128)(2,1)}) %all-gather.23.cloned.1.call-update) | async-done | bytes 21233680 | tf_op jit(solution)/shard_map/all_gather | solution.py:130
  350.8 11.4 fusion.110
  362.2 100.3 %all-gather.25.cloned.1.call-done = bf16[2304,4608]{1,0:T(8,128)(2,1)} async-done(((bf16[144,4608]{1,0:T(8,128)(2,1)}), bf16[2304,4608]{1,0:T(8,128)(2,1)}) %all-gather.25.cloned.1.call-update) | async-done | bytes 21233680 | tf_op jit(solution)/shard_map/all_gather | solution.py:131
  462.4 14.7 multiply_convert_fusion.1
  477.2 96.9 %all-gather.27.cloned.1.call-done = bf16[2304,4608]{1,0:T(8,128)(2,1)} async-done(((bf16[144,4608]{1,0:T(8,128)(2,1)}), bf16[2304,4608]{1,0:T(8,128)(2,1)}) %all-gather.27.cloned.1.call-update) | async-done | bytes 21233680 | tf_op jit(solution)/shard_map/all_gather | solution.py:132
  574.0 12.6 fusion.111
  586.8 28.4 %reduce-scatter.11.cloned.1.call-done = f32[96,2304]{1,0:T(8,128)} async-done(((f32[192,2304]{1,0:T(8,128)}), f32[96,2304]{1,0:T(8,128)}) %reduce-scatter.11.cloned.1.call-update) | async-done | bytes 884752 | tf_op jit(solution)/shard_map/reduce_scatter | solution.py:187
  622.2 12.9 all_gather.79
  635.1 95.9 %all-gather.29.cloned.1.call-done = bf16[2304,4608]{1,0:T(8,128)(2,1)} async-done(((bf16[144,4608]{1,0:T(8,128)(2,1)}), bf16[2304,4608]{1,0:T(8,128)(2,1)}) %all-gather.29.cloned.1.call-update) | async-done | bytes 21233680 | tf_op jit(solution)/shard_map/all_gather | solution.py:216
  731.0 14.2 multiply_convert_fusion
  745.2 97.4 %all-gather.31.cloned.1.call-done = bf16[2304,4608]{1,0:T(8,128)(2,1)} async-done(((bf16[144,4608]{1,0:T(8,128)(2,1)}), bf16[2304,4608]{1,0:T(8,128)(2,1)}) %all-gather.31.cloned.1.call-update) | async-done | bytes 21233680 | tf_op jit(solution)/shard_map/all_gather | solution.py:214
  842.6 12.6 fusion.112
  855.2 98.8 %all-gather.33.cloned.1.call-done = bf16[2304,4608]{1,0:T(8,128)(2,1)} async-done(((bf16[144,4608]{1,0:T(8,128)(2,1)}), bf16[2304,4608]{1,0:T(8,128)(2,1)}) %all-gather.33.cloned.1.call-update) | async-done | bytes 21233680 | tf_op jit(solution)/shard_map/all_gather | solution.py:215
  954.1 13.1 convolution_add_fusion.2
  969.6 26.1 reduce-scatter.13.cloned.1.call-done
  1000.8 12.6 all_gather.83
  1013.4 37.5 %all-gather.35.cloned.1.call-done = bf16[2304,1024]{1,0:T(8,128)(2,1)} async-done(((bf16[144,1024]{1,0:T(8,128)(2,1)}), bf16[2304,1024]{1,0:T(8,128)(2,1)}) %all-gather.35.cloned.1.call-update) | async-done | bytes 4718608 | tf_op jit(solution)/shard_map/all_gather | solution.py:213
  1051.0 4.2 convolution_convert_fusion
  1058.8 2.3 convolution_bitcast_fusion.2
  1061.9 3.1 fusion.39
  1067.1 37.7 %all-gather.37.cloned.1.call-done = bf16[2304,1024]{1,0:T(8,128)(2,1)} async-done(((bf16[144,1024]{1,0:T(8,128)(2,1)}), bf16[2304,1024]{1,0:T(8,128)(2,1)}) %all-gather.37.cloned.1.call-update) | async-done | bytes 4718608 | tf_op jit(solution)/shard_map/all_gather | solution.py:210
  1104.8 5.3 fusion.113
  1110.1 37.7 %all-gather.39.cloned.1.call-done = bf16[2304,512]{1,0:T(8,128)(2,1)} async-done(((bf16[144,512]{1,0:T(8,128)(2,1)}), bf16[2304,512]{1,0:T(8,128)(2,1)}) %all-gather.39.cloned.1.call-update) | async-done | bytes 2359312 | tf_op jit(solution)/shard_map/all_gather | solution.py:211
  1147.8 3.2 convolution_add_fusion.1
  1151.1 5.0 fusion.114
  1156.1 8.0 fusion.44
  1164.1 26.9 all-gather.41.cloned.1.call-done
  1191.0 3.5 fusion.1
  1194.6 18.8 pad_maximum_fusion.1
  1213.4 27.7 %copy.111 = f32[2304,3072]{1,0:T(8,128)} copy(f32[2304,3072]{0,1:T(8,128)} %pad_maximum_fusion.1) | data formatting | bytes 56623104
  1242.3 27.8 %fusion.115 = f32[2304,4608]{1,0:T(8,128)} fusion(bf16[192,2304]{1,0:T(8,128)(2,1)S(1)} %copy-done.6, bf16[192,4608]{1,0:T(8,128)(2,1)} %get-tuple-element.129), kind=kOutput, calls=%fused_computation.171 | convolution fusion | flops 4076863488 | bytes 45121536 | tf_op jit(solution)/shard_map/dot_general | solution.py:20
  1270.1 32.5 %fusion.9 = f32[2304,9216]{1,0:T(8,128)} fusion(bf16[192,2304]{1,0:T(8,128)(2,1)S(1)} %copy-done.9, bf16[192,4608]{1,0:T(8,128)(2,1)S(1)} %copy-done.17, bf16[192,4608]{1,0:T(8,128)(2,1)S(1)} %copy-done.18), kind=kOutput, calls=%fused_computation.16 | convolution fusion | flops 8160804864 | bytes 89358336 | tf_op jit(solution)/shard_map/dot_general | solution.py:20
  1302.7 85.6 %pad_maximum_fusion = f32[2304,13824]{1,0:T(8,128)} fusion(f32[2304,4608]{1,0:T(8,128)} %fusion.115, f32[2304,9216]{1,0:T(8,128)} %fusion.9), kind=kLoop, calls=%fused_computation.1 | loop fusion | flops 31850496 | bytes 254803968 | tf_op jit(solution)/shard_map/concatenate | solution.py:230
  1390.7 40.4 %all-reduce.4 = (f32[2304]{0:T(1024)S(1)}, f32[2304]{0:T(1024)S(1)}, f32[2304]{0:T(1024)S(1)}, f32[2304]{0:T(1024)S(1)}) all-reduce(f32[2304]{0:T(1024)S(1)} %get-tuple-element.87, f32[2304]{0:T(1024)S(1)} %copy-done.40, f32[2304]{0:T(1024)S(1)} %copy-done.39, f32[2304]{0:T(1024)S(1)} %copy-done.38), channel_id=1, replica_groups=mesh['fsdp'=16,'tp'=2] {'fsdp','tp'}, use_global_device_ids=true, to_apply=%region_19.20 | all-reduce | flops 9216 | bytes 73728 | tf_op jit(solution)/shard_map/psum | solution.py:320
  1436.0 76.9 %reduce-scatter.19.cloned.1.call-done = f32[144,3072]{1,0:T(8,128)} async-done(((f32[2304,3072]{1,0:T(8,128)}), f32[144,3072]{1,0:T(8,128)}) %reduce-scatter.19.cloned.1.call-update) | async-done | bytes 1769488
  1514.8 2.4 fusion.103
  1517.2 1177.5 %reduce-scatter.17.cloned.1.call-done = f32[144,13824]{1,0:T(8,128)} async-done(((f32[2304,13824]{1,0:T(8,128)}), f32[144,13824]{1,0:T(8,128)}) %reduce-scatter.17.cloned.1.call-update) | async-done | bytes 7962640 | tf_op jit(solution)/shard_map/reduce_scatter | solution.py:229
  2694.7 6.8 fusion.102
  (212 shorter events, 53.8 us)
Async XLA Ops:
  7.2 85.1 %copy-start.47 = (s32[1,9]{1,0:T(1,128)S(1)}, s32[1,9]{1,0:T(1,128)}, u32[]{:S(2)}) copy-start(s32[1,9]{1,0:T(1,128)} %param.15) | copy-start | bytes 112
  7.2 85.8 %all-gather.17.cloned.1.call-start = ((), (), s32[]{:S(2)}) async-start(), calls=%async_computation.7 | async-start | bytes 2506752 | tf_op jit(solution)/shard_map/all_gather | solution.py:123
  7.9 91.1 %all-gather.15.cloned.1.call-start = ((), (), s32[]{:S(2)}) async-start(), calls=%async_computation.6 | async-start | bytes 2506752 | tf_op jit(solution)/shard_map/all_gather | solution.py:124
  8.7 144.5 %all-gather.19.cloned.1.call-start = ((), (), s32[]{:S(2)}) async-start(), calls=%async_computation.8 | async-start | bytes 5013504 | tf_op jit(solution)/shard_map/all_gather | solution.py:122
  9.4 197.6 %all-gather.21.cloned.1.call-start = ((), (), s32[]{:S(2)}) async-start(), calls=%async_computation.9 | async-start | bytes 5013504 | tf_op jit(solution)/shard_map/all_gather | solution.py:125
  10.0 229.3 %reduce-scatter.9.cloned.1.call-start = ((), (), s32[]{:S(2)}) async-start(), calls=%async_computation.10 | async-start | bytes 2654208 | tf_op jit(solution)/shard_map/reduce_scatter | solution.py:175
  79.2 13.7 copy-start.27
  92.5 65.4 %copy-start.29 = (pred[192,192]{0,1:T(8,128)(4,1)}, pred[192,192]{0,1:T(8,128)(4,1)S(1)}, u32[]{:S(2)}) copy-start(pred[192,192]{0,1:T(8,128)(4,1)S(1)} %fusion.77) | copy-start | bytes 110596
  92.9 64.0 %copy-start.10 = (f32[192,128]{1,0:T(8,128)}, f32[192,128]{1,0:T(8,128)S(1)}, u32[]{:S(2)}) copy-start(f32[192,128]{1,0:T(8,128)S(1)} %get-tuple-element.125) | copy-start | bytes 294916
  92.9 64.0 %copy-start.12 = (f32[192,128]{1,0:T(8,128)}, f32[192,128]{1,0:T(8,128)S(1)}, u32[]{:S(2)}) copy-start(f32[192,128]{1,0:T(8,128)S(1)} %get-tuple-element.126) | copy-start | bytes 294916
  101.3 56.6 %copy-start.25 = (bf16[192,2,256]{2,1,0:T(2,128)(2,1)}, bf16[192,2,256]{2,1,0:T(2,128)(2,1)S(1)}, u32[]{:S(2)}) copy-start(bf16[192,2,256]{2,1,0:T(2,128)(2,1)S(1)} %reshape.267) | copy-start | bytes 589828
  101.6 55.7 %copy-start.35 = (bf16[192,2,128]{2,0,1:T(8,128)(2,1)}, bf16[192,2,128]{2,0,1:T(8,128)(2,1)S(1)}, u32[]{:S(2)}) copy-start(bf16[192,2,128]{2,0,1:T(8,128)(2,1)S(1)} %get-tuple-element.121) | copy-start | bytes 294916
  101.6 55.7 %copy-start.37 = (bf16[192,2,128]{2,0,1:T(8,128)(2,1)}, bf16[192,2,128]{2,0,1:T(8,128)(2,1)S(1)}, u32[]{:S(2)}) copy-start(bf16[192,2,128]{2,0,1:T(8,128)(2,1)S(1)} %get-tuple-element.122) | copy-start | bytes 294916
  157.9 54.3 %copy-start.45 = (f32[2,2,192]{2,1,0:T(2,128)}, f32[2,2,192]{2,1,0:T(2,128)S(1)}, u32[]{:S(2)}) copy-start(f32[2,2,192]{2,1,0:T(2,128)S(1)} %log_add_fusion) | copy-start | bytes 9220
  159.2 53.0 %copy-start.19 = (bf16[192,1024]{1,0:T(8,128)(2,1)}, bf16[192,1024]{1,0:T(8,128)(2,1)S(1)}, u32[]{:S(2)}) copy-start(bf16[192,1024]{1,0:T(8,128)(2,1)S(1)} %convert_element_type.109) | copy-start | bytes 1179652
  212.2 28.4 %copy-start.1 = (bf16[96,2304]{1,0:T(8,128)(2,1)S(1)}, bf16[96,2304]{1,0:T(8,128)(2,1)}, u32[]{:S(2)}) copy-start(bf16[96,2304]{1,0:T(8,128)(2,1)} %param.14) | copy-start | bytes 1327108
  212.3 138.5 %all-gather.23.cloned.1.call-start = ((), (), s32[]{:S(2)}) async-start(), calls=%async_computation.11 | async-start | bytes 22560768 | tf_op jit(solution)/shard_map/all_gather | solution.py:130
  212.8 249.6 %all-gather.25.cloned.1.call-start = ((), (), s32[]{:S(2)}) async-start(), calls=%async_computation.12 | async-start | bytes 22560768 | tf_op jit(solution)/shard_map/all_gather | solution.py:131
  213.6 360.4 %all-gather.27.cloned.1.call-start = ((), (), s32[]{:S(2)}) async-start(), calls=%async_computation.13 | async-start | bytes 22560768 | tf_op jit(solution)/shard_map/all_gather | solution.py:132
  214.3 400.8 %reduce-scatter.11.cloned.1.call-start = ((), (), s32[]{:S(2)}) async-start(), calls=%async_computation.14 | async-start | bytes 2654208 | tf_op jit(solution)/shard_map/reduce_scatter | solution.py:187
  214.4 27.8 %copy-start.33 = (f32[2304]{0:T(1024)}, f32[2304]{0:T(1024)S(1)}, u32[]{:S(2)}) copy-start(f32[2304]{0:T(1024)S(1)} %convert_element_type.111) | copy-start | bytes 27652
  255.1 207.4 %copy-start.8 = (bf16[192,2304]{1,0:T(8,128)(2,1)}, bf16[192,2304]{1,0:T(8,128)(2,1)S(1)}, u32[]{:S(2)}) copy-start(bf16[192,2304]{1,0:T(8,128)(2,1)S(1)} %all_gather.74) | copy-start | bytes 2654212
  574.0 42.5 %copy-start.7 = (bf16[96,2304]{1,0:T(8,128)(2,1)S(1)}, bf16[96,2304]{1,0:T(8,128)(2,1)}, u32[]{:S(2)}) copy-start(bf16[96,2304]{1,0:T(8,128)(2,1)} %param.27) | copy-start | bytes 1327108
  586.7 144.3 %all-gather.29.cloned.1.call-start = ((), (), s32[]{:S(2)}) async-start(), calls=%async_computation.15 | async-start | bytes 22560768 | tf_op jit(solution)/shard_map/all_gather | solution.py:216
  620.8 221.8 %all-gather.31.cloned.1.call-start = ((), (), s32[]{:S(2)}) async-start(), calls=%async_computation.16 | async-start | bytes 22560768 | tf_op jit(solution)/shard_map/all_gather | solution.py:214
  621.5 332.5 %all-gather.33.cloned.1.call-start = ((), (), s32[]{:S(2)}) async-start(), calls=%async_computation.17 | async-start | bytes 22560768 | tf_op jit(solution)/shard_map/all_gather | solution.py:215
  622.1 373.6 %reduce-scatter.13.cloned.1.call-start = ((), (), s32[]{:S(2)}) async-start(), calls=%async_computation.18 | async-start | bytes 2654208 | tf_op jit(solution)/shard_map/reduce_scatter | solution.py:239
  635.1 110.1 %copy-start.5 = (bf16[192,2304]{1,0:T(8,128)(2,1)}, bf16[192,2304]{1,0:T(8,128)(2,1)S(1)}, u32[]{:S(2)}) copy-start(bf16[192,2304]{1,0:T(8,128)(2,1)S(1)} %all_gather.79) | copy-start | bytes 2654212
  954.1 41.6 %copy-start.34 = (f32[2304]{0:T(1024)S(1)}, f32[2304]{0:T(1024)}, u32[]{:S(2)}) copy-start(f32[2304]{0:T(1024)} %copy-done.33) | copy-start | bytes 27652
  967.2 30.5 %copy-start = (f32[96,2304]{1,0:T(8,128)S(1)}, f32[96,2304]{1,0:T(8,128)}, u32[]{:S(2)}) copy-start(f32[96,2304]{1,0:T(8,128)} %reduce-scatter.9.cloned.1.call-done) | copy-start | bytes 2654212
  967.2 30.5 %copy-start.44 = (f32[96]{0:T(128)S(1)}, f32[96]{0:T(128)}, u32[]{:S(2)}) copy-start(f32[96]{0:T(128)} %copy-done.43) | copy-start | bytes 1156
  967.2 83.7 %all-gather.35.cloned.1.call-start = ((), (), s32[]{:S(2)}) async-start(), calls=%async_computation.19 | async-start | bytes 5013504 | tf_op jit(solution)/shard_map/all_gather | solution.py:213
  967.8 137.0 %all-gather.37.cloned.1.call-start = ((), (), s32[]{:S(2)}) async-start(), calls=%async_computation.20 | async-start | bytes 5013504 | tf_op jit(solution)/shard_map/all_gather | solution.py:210
  968.4 179.4 %all-gather.39.cloned.1.call-start = ((), (), s32[]{:S(2)}) async-start(), calls=%async_computation.21 | async-start | bytes 2506752 | tf_op jit(solution)/shard_map/all_gather | solution.py:211
  969.0 222.0 %all-gather.41.cloned.1.call-start = ((), (), s32[]{:S(2)}) async-start(), calls=%async_computation.22 | async-start | bytes 2506752 | tf_op jit(solution)/shard_map/all_gather | solution.py:212
  969.6 418.8 %reduce-scatter.15.cloned.1.call-start = ((), (), s32[]{:S(2)}) async-start(), calls=%async_computation.23 | async-start | bytes 1327104 | tf_op jit(solution)/shard_map/reduce_scatter | solution.py:310
  1013.4 43.0 %copy-start.24 = (f32[2,192,192,2]{2,1,3,0:T(8,128)S(1)}, f32[2,192,192,2]{2,1,3,0:T(8,128)}, u32[]{:S(2)}) copy-start(f32[2,192,192,2]{2,1,3,0:T(8,128)} %copy-done.23) | copy-start | bytes 1769476
  1013.4 43.0 %copy-start.30 = (pred[192,192]{0,1:T(8,128)(4,1)S(1)}, pred[192,192]{0,1:T(8,128)(4,1)}, u32[]{:S(2)}) copy-start(pred[192,192]{0,1:T(8,128)(4,1)} %copy-done.29) | copy-start | bytes 110596
  1013.4 43.0 %copy-start.46 = (f32[2,2,192]{2,1,0:T(2,128)S(1)}, f32[2,2,192]{2,1,0:T(2,128)}, u32[]{:S(2)}) copy-start(f32[2,2,192]{2,1,0:T(2,128)} %copy-done.45) | copy-start | bytes 9220
  1013.4 44.2 %copy-start.26 = (bf16[192,2,256]{2,1,0:T(2,128)(2,1)S(1)}, bf16[192,2,256]{2,1,0:T(2,128)(2,1)}, u32[]{:S(2)}) copy-start(bf16[192,2,256]{2,1,0:T(2,128)(2,1)} %copy-done.25) | copy-start | bytes 589828
  1067.1 43.0 %copy-start.21 = (bf16[24,8,4,256]{3,1,2,0:T(8,128)(2,1)}, bf16[24,8,4,256]{3,1,2,0:T(8,128)(2,1)S(1)}, u32[]{:S(2)}) copy-start(bf16[24,8,4,256]{3,1,2,0:T(8,128)(2,1)S(1)} %copy.123) | copy-start | bytes 1179652
  1156.1 34.9 %copy-start.15 = (bf16[2,24,8,256]{3,2,0,1:T(8,128)(2,1)S(1)}, bf16[2,24,8,256]{3,2,0,1:T(8,128)(2,1)}, u32[]{:S(2)}) copy-start(bf16[2,24,8,256]{3,2,0,1:T(8,128)(2,1)} %copy.122) | copy-start | bytes 589828
  1194.6 318.4 %reduce-scatter.19.cloned.1.call-start = ((), (), s32[]{:S(2)}) async-start(), calls=%async_computation.25 | async-start | bytes 30081024
  1241.2 28.9 %copy-start.9 = (bf16[192,2304]{1,0:T(8,128)(2,1)S(1)}, bf16[192,2304]{1,0:T(8,128)(2,1)}, u32[]{:S(2)}) copy-start(bf16[192,2304]{1,0:T(8,128)(2,1)} %copy-done.8) | copy-start | bytes 2654212
  1241.2 28.9 %copy-start.17 = (bf16[192,4608]{1,0:T(8,128)(2,1)S(1)}, bf16[192,4608]{1,0:T(8,128)(2,1)}, u32[]{:S(2)}) copy-start(bf16[192,4608]{1,0:T(8,128)(2,1)} %get-tuple-element.105) | copy-start | bytes 5308420
  1241.2 1453.5 %reduce-scatter.17.cloned.1.call-start = ((), (), s32[]{:S(2)}) async-start(), calls=%async_computation.24 | async-start | bytes 135364608 | tf_op jit(solution)/shard_map/reduce_scatter | solution.py:229
  1242.3 27.8 %copy-start.18 = (bf16[192,4608]{1,0:T(8,128)(2,1)S(1)}, bf16[192,4608]{1,0:T(8,128)(2,1)}, u32[]{:S(2)}) copy-start(bf16[192,4608]{1,0:T(8,128)(2,1)} %get-tuple-element.106) | copy-start | bytes 5308420
  1388.3 45.4 %copy-start.4 = (f32[96,2304]{1,0:T(8,128)S(1)}, f32[96,2304]{1,0:T(8,128)}, u32[]{:S(2)}) copy-start(f32[96,2304]{1,0:T(8,128)} %copy-done.3) | copy-start | bytes 2654212
  (20 other events, 63.1 us)
Sparse Core Ops, SparseCore 0:
  10.3 45.2 all-gather.16
  57.8 41.0 all-gather.14
  101.3 51.8 all-gather.18
  155.3 51.6 all-gather.20
  212.4 26.8 reduce-scatter.8
  240.7 110.0 all-gather.22
  352.4 109.9 all-gather.24
  464.0 109.9 all-gather.26
  586.8 28.2 reduce-scatter.10
  620.9 109.9 all-gather.28
  732.6 109.9 all-gather.30
  844.0 109.9 all-gather.32
  967.3 28.2 reduce-scatter.12
  997.8 53.1 all-gather.34
  1053.1 51.6 all-gather.36
  1106.9 40.8 all-gather.38
  1150.0 41.0 all-gather.40
  1194.7 17.3 reduce-scatter.14
  1241.3 271.5 reduce-scatter.18
  1517.0 1177.6 reduce-scatter.16
where the time goes:
time: 2720 us; the launch traced here: 2710 us
  waiting for transfers between devices  2170 us (80%)
  matrix products  189 us (7%)
  blocking collectives  151 us (6%)
  other arithmetic  127 us (5%)
  local copies, waits for them, and re-layouts  54.3 us (2%)
    reduce_scatter x1, waiting for transfers between devices, shards(): lax.psum_scatter(jnp.concatenate([contract_first(left_rows, gate_up_grad)...  1180 us
    all_gather x1, waiting for transfers between devices, shards(): lax.all_gather(up_weight, 'fsdp', axis=0, tiled=True)  100 us
    all_gather x1, waiting for transfers between devices, shards(): lax.all_gather(held_back[5], 'fsdp', axis=0, tiled=True)  98.8 us
    all_gather x1, waiting for transfers between devices, shards(): lax.all_gather(held_back[4], 'fsdp', axis=0, tiled=True)  97.4 us
    all_gather x1, waiting for transfers between devices, shards(): lax.all_gather(down_weight, 'fsdp', axis=0, tiled=True)  96.9 us
    all_gather x1, waiting for transfers between devices, shards(): lax.all_gather(held_back[6], 'fsdp', axis=0, tiled=True)  95.9 us
    all_gather x1, waiting for transfers between devices, shards(): lax.all_gather(gate_weight, 'fsdp', axis=0, tiled=True)  95.7 us
    concatenate x1, other arithmetic, shards(): jnp.concatenate([contract_first(left_rows, gate_up_grad), contract_first(...  85.6 us
  transfers between devices with their start and end apart: 20, of which 18 were waited for; matrix products, arithmetic and copies ran while one was open for 12% of the time, Pallas kernels for 0%

commit v1 on v0

--- a/solution.py
+++ b/solution.py
@@ -3,11 +3,40 @@
 import jax.numpy as jnp
 from jax import lax
 from jax.sharding import PartitionSpec as P
+from jax.lax import axis_index, axis_size, ppermute
 
 HEAD_SIZE = 256
 EPSILON = 1e-06
 SOFTCAP = 50.0
 NEGATIVE = -1e30
+
+
+def wait_sites(local_x, named_axis):
+    y, top, wide_out = (axis_size(named_axis), axis_index(named_axis), local_x.shape[0])
+    block_list = []
+    for pp, b in enumerate(local_x.shape):
+        block_list.append(b * y if pp == 0 else b)
+    item_now = lax.dynamic_update_slice_in_dim(
+        jnp.zeros(block_list, local_x.dtype), local_x, top * wide_out, axis=0
+    )
+    v_now = then = local_x
+    for m in range(1, y // 2 + 1):
+        copies = []
+        for pp in range(y):
+            copies.append((pp, (pp + 1) % y))
+        v_now = ppermute(v_now, axis_name=named_axis, perm=copies)
+        item_now = lax.dynamic_update_slice_in_dim(
+            item_now, v_now, (top - m) % y * wide_out, axis=0
+        )
+        if 2 * m < y:
+            found = []
+            for pp in range(y):
+                found.append((pp, (pp - 1) % y))
+            then = ppermute(then, axis_name=named_axis, perm=found)
+            item_now = lax.dynamic_update_slice_in_dim(
+                item_now, then, (top + m) % y * wide_out, axis=0
+            )
+    return item_now
 
 
 def contract_last(left_rows, right_rows):
@@ -127,7 +156,7 @@
         lax.all_gather(attention_post_gain, "fsdp", axis=0, tiled=True),
     )
     gate_full, up_full, down_full, gain_three, gain_four = (
-        lax.all_gather(gate_weight, "fsdp", axis=0, tiled=True),
+        wait_sites(gate_weight, "fsdp"),
         lax.all_gather(up_weight, "fsdp", axis=0, tiled=True),
         lax.all_gather(down_weight, "fsdp", axis=0, tiled=True),
         lax.all_gather(feedforward_norm_gain, "fsdp", axis=0, tiled=True),

time: 2720 us -> 2810 us (1.033)
  starting transfers between devices: 0.99 us -> 281 us
  waiting for transfers between devices: 2170 us -> 1950 us
  local copies, waits for them, and re-layouts: 54.3 us -> 89.2 us
    ppermute x0 -> x15, starting transfers between devices: none -> 280 us  [the longest x8 275 us: wait_sites(): v_now = ppermute(v_now, axis_name=named_axis, perm=copies)]
    all_gather x1, waiting for transfers between devices: 100 us -> 0.01 us  [shards(): lax.all_gather(up_weight, 'fsdp', axis=0, tiled=True)]
    all_gather x1, waiting for transfers between devices: 96.9 us -> 0.01 us  [shards(): lax.all_gather(down_weight, 'fsdp', axis=0, tiled=True)]
    all_gather x1 -> x0, waiting for transfers between devices: 95.7 us -> none  [shards(): lax.all_gather(gate_weight, 'fsdp', axis=0, tiled=True)]
    ppermute x0 -> x15, waiting for transfers between devices: none -> 82.3 us  [the longest x8 82.3 us: wait_sites(): v_now = ppermute(v_now, axis_name=named_axis, perm=copies)]
    unnamed x21 -> x20, waiting for transfers between devices: 84.9 us -> 84.1 us
  transfers between devices with their start and end apart: 20 -> 34, of which waited for: 18 -> 21; matrix products, arithmetic and copies ran while one was open for 12% -> 13% of each run, Pallas kernels for 0% -> 0%
where the time goes in v1:
time: 2810 us; the launch traced here: 2800 us
  waiting for transfers between devices  1950 us (69%)
  starting transfers between devices  281 us (10%)
  matrix products  190 us (7%)
  blocking collectives  148 us (5%)
  other arithmetic  127 us (5%)
  local copies, waits for them, and re-layouts  89.2 us (3%)
    reduce_scatter x1, waiting for transfers between devices, shards(): lax.psum_scatter(jnp.concatenate([contract_first(left_rows, gate_up_grad)...  1180 us
    ppermute x8, starting transfers between devices, wait_sites(): v_now = ppermute(v_now, axis_name=named_axis, perm=copies)  275 us
    all_gather x1, waiting for transfers between devices, shards(): lax.all_gather(held_back[5], 'fsdp', axis=0, tiled=True)  99 us
    all_gather x1, waiting for transfers between devices, shards(): lax.all_gather(held_back[4], 'fsdp', axis=0, tiled=True)  97.2 us
    all_gather x1, waiting for transfers between devices, shards(): lax.all_gather(held_back[6], 'fsdp', axis=0, tiled=True)  96.2 us
    concatenate x1, other arithmetic, shards(): jnp.concatenate([contract_first(left_rows, gate_up_grad), contract_first(...  85.8 us
    unnamed x20, waiting for transfers between devices  84.1 us
    ppermute x8, waiting for transfers between devices, wait_sites(): v_now = ppermute(v_now, axis_name=named_axis, perm=copies)  82.3 us
  transfers between devices with their start and end apart: 34, of which 21 were waited for; matrix products, arithmetic and copies ran while one was open for 13% of the time, Pallas kernels for 0%

profile of v1, /device:TPU:0, one launch (start us, length us, event | category | flops | bytes accessed | tf_op | source)
XLA Modules:
  0.0 2802.7 jit_solution(16302443292058600138)
XLA Ops:
  15.4 63.9 %all-reduce.5 = (bf16[2304]{0:T(1024)(128)(2,1)S(1)}, bf16[2304]{0:T(1024)(128)(2,1)S(1)}, bf16[2304]{0:T(1024)(128)(2,1)S(1)}, bf16[2304]{0:T(1024)(128)(2,1)S(1)}) all-reduce(bf16[2304]{0:T(1024)(128)(2,1)S(1)} %dynamic-update-slice, bf16[2304]{0:T(1024)(128)(2,1)S(1)} %dynamic-update-slice.1, ...), channel_id=1, replica_groups=mesh['fsdp'=16,'tp'=2] {'fsdp'}, use_global_device_ids=true, to_apply=%add | all-reduce | flops 9216 | bytes 36864
  83.3 9.0 all_gather.64
  101.6 51.6 %all-gather.18.cloned.1.call-done = bf16[2304,1024]{1,0:T(8,128)(2,1)} async-done(((bf16[144,1024]{1,0:T(8,128)(2,1)}), bf16[2304,1024]{1,0:T(8,128)(2,1)}) %all-gather.18.cloned.1.call-update) | async-done | bytes 4718608 | tf_op jit(solution)/shard_map/all_gather | solution.py:151
  159.3 47.7 %all-gather.20.cloned.1.call-done = bf16[2304,1024]{1,0:T(8,128)(2,1)} async-done(((bf16[144,1024]{1,0:T(8,128)(2,1)}), bf16[2304,1024]{1,0:T(8,128)(2,1)}) %all-gather.20.cloned.1.call-update) | async-done | bytes 4718608 | tf_op jit(solution)/shard_map/all_gather | solution.py:154
  207.0 5.2 fusion.109
  218.1 15.6 collective-permute-done
  233.7 9.6 collective-permute-start.2
  244.4 12.3 collective-permute-done.2
  256.7 51.6 %collective-permute-start.4 = (bf16[144,4608]{1,0:T(8,128)(2,1)}, bf16[144,4608]{1,0:T(8,128)(2,1)}, u32[]{:S(2)}, u32[]{:S(2)}) collective-permute-start(bf16[144,4608]{1,0:T(8,128)(2,1)} %collective-permute-done.2), channel_id=1, source_target_pairs={{0,2},{2,4},{4,6},{6,8},{8,10},{10,12},{12,14},{14,16},{16,18},{18... | collective-permute-start | bytes 3981320 | tf_op jit(solution)/shard_map/ppermute | solution.py:27
  308.3 17.1 collective-permute-done.4
  325.5 42.7 %collective-permute-start.6 = (bf16[144,4608]{1,0:T(8,128)(2,1)}, bf16[144,4608]{1,0:T(8,128)(2,1)}, u32[]{:S(2)}, u32[]{:S(2)}) collective-permute-start(bf16[144,4608]{1,0:T(8,128)(2,1)} %collective-permute-done.4), channel_id=1, source_target_pairs={{0,2},{2,4},{4,6},{6,8},{8,10},{10,12},{12,14},{14,16},{16,18},{18... | collective-permute-start | bytes 3981320 | tf_op jit(solution)/shard_map/ppermute | solution.py:27
  368.2 7.3 broadcast_in_dim.44
  380.5 15.0 collective-permute-done.6
  395.5 39.8 %collective-permute-start.8 = (bf16[144,4608]{1,0:T(8,128)(2,1)}, bf16[144,4608]{1,0:T(8,128)(2,1)S(1)}, u32[]{:S(2)}, u32[]{:S(2)}) collective-permute-start(bf16[144,4608]{1,0:T(8,128)(2,1)} %collective-permute-done.6), channel_id=1, source_target_pairs={{0,2},{2,4},{4,6},{6,8},{8,10},{10,12},{12,14},{14,16},{16,18},{18... | collective-permute-start | bytes 3981320 | tf_op jit(solution)/shard_map/ppermute | solution.py:27
  442.7 45.6 %collective-permute-start.10 = (bf16[144,4608]{1,0:T(8,128)(2,1)S(1)}, bf16[144,4608]{1,0:T(8,128)(2,1)S(1)}, u32[]{:S(2)}, u32[]{:S(2)}) collective-permute-start(bf16[144,4608]{1,0:T(8,128)(2,1)S(1)} %collective-permute-done.8), channel_id=1, source_target_pairs={{0,2},{2,4},{4,6},{6,8},{8,10},{10,12},{12,14},{14,16},{16,18},{18... | collective-permute-start | bytes 3981320 | tf_op jit(solution)/shard_map/ppermute | solution.py:27
  494.5 10.1 collective-permute-done.10
  504.6 43.5 %collective-permute-start.12 = (bf16[144,4608]{1,0:T(8,128)(2,1)S(1)}, bf16[144,4608]{1,0:T(8,128)(2,1)S(1)}, u32[]{:S(2)}, u32[]{:S(2)}) collective-permute-start(bf16[144,4608]{1,0:T(8,128)(2,1)S(1)} %collective-permute-done.10), channel_id=1, source_target_pairs={{0,2},{2,4},{4,6},{6,8},{8,10},{10,12},{12,14},{14,16},{16,18},{18... | collective-permute-start | bytes 3981320 | tf_op jit(solution)/shard_map/ppermute | solution.py:27
  551.8 42.3 %collective-permute-start.14 = (bf16[144,4608]{1,0:T(8,128)(2,1)S(1)}, bf16[144,4608]{1,0:T(8,128)(2,1)S(1)}, u32[]{:S(2)}, u32[]{:S(2)}) collective-permute-start(bf16[144,4608]{1,0:T(8,128)(2,1)S(1)} %collective-permute-done.12), channel_id=1, source_target_pairs={{0,2},{2,4},{4,6},{6,8},{8,10},{10,12},{12,14},{14,16},{16,18},{18... | collective-permute-start | bytes 3981320 | tf_op jit(solution)/shard_map/ppermute | solution.py:27
  597.5 12.0 collective-permute-done.14
  613.7 9.0 all_gather.71
  622.7 11.9 fusion.110
  634.6 14.7 multiply_convert_fusion.1
  649.3 12.6 fusion.111
  662.1 48.0 %reduce-scatter.11.cloned.1.call-done = f32[96,2304]{1,0:T(8,128)} async-done(((f32[192,2304]{1,0:T(8,128)}), f32[96,2304]{1,0:T(8,128)}) %reduce-scatter.11.cloned.1.call-update) | async-done | bytes 884752 | tf_op jit(solution)/shard_map/reduce_scatter | solution.py:216
  717.1 12.6 all_gather.75
  729.7 96.2 %all-gather.26.cloned.1.call-done = bf16[2304,4608]{1,0:T(8,128)(2,1)} async-done(((bf16[144,4608]{1,0:T(8,128)(2,1)}), bf16[2304,4608]{1,0:T(8,128)(2,1)}) %all-gather.26.cloned.1.call-update) | async-done | bytes 21233680 | tf_op jit(solution)/shard_map/all_gather | solution.py:245
  825.9 14.2 multiply_convert_fusion
  840.1 97.2 %all-gather.28.cloned.1.call-done = bf16[2304,4608]{1,0:T(8,128)(2,1)} async-done(((bf16[144,4608]{1,0:T(8,128)(2,1)}), bf16[2304,4608]{1,0:T(8,128)(2,1)}) %all-gather.28.cloned.1.call-update) | async-done | bytes 21233680 | tf_op jit(solution)/shard_map/all_gather | solution.py:243
  937.3 12.6 fusion.112
  950.0 99.0 %all-gather.30.cloned.1.call-done = bf16[2304,4608]{1,0:T(8,128)(2,1)} async-done(((bf16[144,4608]{1,0:T(8,128)(2,1)}), bf16[2304,4608]{1,0:T(8,128)(2,1)}) %all-gather.30.cloned.1.call-update) | async-done | bytes 21233680 | tf_op jit(solution)/shard_map/all_gather | solution.py:244
  1049.0 13.1 convolution_add_fusion.2
  1064.6 25.9 reduce-scatter.13.cloned.1.call-done
  1095.7 12.7 all_gather.79
  1108.4 37.6 %all-gather.32.cloned.1.call-done = bf16[2304,1024]{1,0:T(8,128)(2,1)} async-done(((bf16[144,1024]{1,0:T(8,128)(2,1)}), bf16[2304,1024]{1,0:T(8,128)(2,1)}) %all-gather.32.cloned.1.call-update) | async-done | bytes 4718608 | tf_op jit(solution)/shard_map/all_gather | solution.py:242
  1162.0 37.8 %all-gather.34.cloned.1.call-done = bf16[2304,1024]{1,0:T(8,128)(2,1)} async-done(((bf16[144,1024]{1,0:T(8,128)(2,1)}), bf16[2304,1024]{1,0:T(8,128)(2,1)}) %all-gather.34.cloned.1.call-update) | async-done | bytes 4718608 | tf_op jit(solution)/shard_map/all_gather | solution.py:239
  1199.8 5.3 fusion.113
  1205.1 37.8 %all-gather.36.cloned.1.call-done = bf16[2304,512]{1,0:T(8,128)(2,1)} async-done(((bf16[144,512]{1,0:T(8,128)(2,1)}), bf16[2304,512]{1,0:T(8,128)(2,1)}) %all-gather.36.cloned.1.call-update) | async-done | bytes 2359312 | tf_op jit(solution)/shard_map/all_gather | solution.py:240
  1251.1 8.0 fusion.44
  1259.2 26.9 all-gather.38.cloned.1.call-done
  1289.6 18.9 pad_maximum_fusion.1
  1308.5 27.7 copy.111
  1337.4 27.8 fusion.115
  1365.2 32.5 %fusion.9 = f32[2304,9216]{1,0:T(8,128)} fusion(bf16[192,2304]{1,0:T(8,128)(2,1)S(1)} %copy-done.10, bf16[192,4608]{1,0:T(8,128)(2,1)S(1)} %copy-done.18, bf16[192,4608]{1,0:T(8,128)(2,1)S(1)} %copy-done.19), kind=kOutput, calls=%fused_computation.16 | convolution fusion | flops 8160804864 | bytes 89358336 | tf_op jit(solution)/shard_map/dot_general | solution.py:49
  1397.7 85.8 %pad_maximum_fusion = f32[2304,13824]{1,0:T(8,128)} fusion(f32[2304,4608]{1,0:T(8,128)} %fusion.115, f32[2304,9216]{1,0:T(8,128)} %fusion.9), kind=kLoop, calls=%fused_computation.1 | loop fusion | flops 31850496 | bytes 254803968 | tf_op jit(solution)/shard_map/concatenate | solution.py:259
  1486.1 40.5 %all-reduce.4 = (f32[2304]{0:T(1024)S(1)}, f32[2304]{0:T(1024)S(1)}, f32[2304]{0:T(1024)S(1)}, f32[2304]{0:T(1024)S(1)}) all-reduce(f32[2304]{0:T(1024)S(1)} %get-tuple-element.87, f32[2304]{0:T(1024)S(1)} %copy-done.44, f32[2304]{0:T(1024)S(1)} %copy-done.43, f32[2304]{0:T(1024)S(1)} %copy-done.42), channel_id=1, replica_groups=mesh['fsdp'=16,'tp'=2] {'fsdp','tp'}, use_global_device_ids=true, to_apply=%region_19.20 | all-reduce | flops 9216 | bytes 73728 | tf_op jit(solution)/shard_map/psum | solution.py:349
  1531.3 76.7 %reduce-scatter.19.cloned.1.call-done = f32[144,3072]{1,0:T(8,128)} async-done(((f32[2304,3072]{1,0:T(8,128)}), f32[144,3072]{1,0:T(8,128)}) %reduce-scatter.19.cloned.1.call-update) | async-done | bytes 1769488
  1612.3 1176.6 %reduce-scatter.17.cloned.1.call-done = f32[144,13824]{1,0:T(8,128)} async-done(((f32[2304,13824]{1,0:T(8,128)}), f32[144,13824]{1,0:T(8,128)}) %reduce-scatter.17.cloned.1.call-update) | async-done | bytes 7962640 | tf_op jit(solution)/shard_map/reduce_scatter | solution.py:258
  2788.9 6.8 fusion.102
  (264 shorter events, 118.3 us)
Async XLA Ops:
  7.2 85.1 %copy-start.51 = (s32[1,9]{1,0:T(1,128)S(1)}, s32[1,9]{1,0:T(1,128)}, u32[]{:S(2)}) copy-start(s32[1,9]{1,0:T(1,128)} %param.15) | copy-start | bytes 112
  7.2 85.8 %all-gather.16.cloned.1.call-start = ((), (), s32[]{:S(2)}) async-start(), calls=%async_computation.7 | async-start | bytes 2506752 | tf_op jit(solution)/shard_map/all_gather | solution.py:152
  7.9 91.1 %all-gather.14.cloned.1.call-start = ((), (), s32[]{:S(2)}) async-start(), calls=%async_computation.6 | async-start | bytes 2506752 | tf_op jit(solution)/shard_map/all_gather | solution.py:153
  8.7 144.5 %all-gather.18.cloned.1.call-start = ((), (), s32[]{:S(2)}) async-start(), calls=%async_computation.8 | async-start | bytes 5013504 | tf_op jit(solution)/shard_map/all_gather | solution.py:151
  9.4 197.6 %all-gather.20.cloned.1.call-start = ((), (), s32[]{:S(2)}) async-start(), calls=%async_computation.9 | async-start | bytes 5013504 | tf_op jit(solution)/shard_map/all_gather | solution.py:154
  10.0 600.7 %reduce-scatter.9.cloned.1.call-start = ((), (), s32[]{:S(2)}) async-start(), calls=%async_computation.10 | async-start | bytes 2654208 | tf_op jit(solution)/shard_map/reduce_scatter | solution.py:204
  92.5 65.4 %copy-start.33 = (pred[192,192]{0,1:T(8,128)(4,1)}, pred[192,192]{0,1:T(8,128)(4,1)S(1)}, u32[]{:S(2)}) copy-start(pred[192,192]{0,1:T(8,128)(4,1)S(1)} %fusion.77) | copy-start | bytes 110596
  92.9 64.0 %copy-start.11 = (f32[192,128]{1,0:T(8,128)}, f32[192,128]{1,0:T(8,128)S(1)}, u32[]{:S(2)}) copy-start(f32[192,128]{1,0:T(8,128)S(1)} %get-tuple-element.125) | copy-start | bytes 294916
  92.9 64.0 %copy-start.13 = (f32[192,128]{1,0:T(8,128)}, f32[192,128]{1,0:T(8,128)S(1)}, u32[]{:S(2)}) copy-start(f32[192,128]{1,0:T(8,128)S(1)} %get-tuple-element.126) | copy-start | bytes 294916
  101.3 56.6 %copy-start.29 = (bf16[192,2,256]{2,1,0:T(2,128)(2,1)}, bf16[192,2,256]{2,1,0:T(2,128)(2,1)S(1)}, u32[]{:S(2)}) copy-start(bf16[192,2,256]{2,1,0:T(2,128)(2,1)S(1)} %reshape.267) | copy-start | bytes 589828
  101.6 55.7 %copy-start.39 = (bf16[192,2,128]{2,0,1:T(8,128)(2,1)}, bf16[192,2,128]{2,0,1:T(8,128)(2,1)S(1)}, u32[]{:S(2)}) copy-start(bf16[192,2,128]{2,0,1:T(8,128)(2,1)S(1)} %get-tuple-element.121) | copy-start | bytes 294916
  101.6 55.7 %copy-start.41 = (bf16[192,2,128]{2,0,1:T(8,128)(2,1)}, bf16[192,2,128]{2,0,1:T(8,128)(2,1)S(1)}, u32[]{:S(2)}) copy-start(bf16[192,2,128]{2,0,1:T(8,128)(2,1)S(1)} %get-tuple-element.122) | copy-start | bytes 294916
  157.9 54.3 %copy-start.49 = (f32[2,2,192]{2,1,0:T(2,128)}, f32[2,2,192]{2,1,0:T(2,128)S(1)}, u32[]{:S(2)}) copy-start(f32[2,2,192]{2,1,0:T(2,128)S(1)} %log_add_fusion) | copy-start | bytes 9220
  159.2 47.8 %copy-start.20 = (bf16[192,1024]{1,0:T(8,128)(2,1)}, bf16[192,1024]{1,0:T(8,128)(2,1)S(1)}, u32[]{:S(2)}) copy-start(bf16[192,1024]{1,0:T(8,128)(2,1)S(1)} %convert_element_type.109) | copy-start | bytes 1179652
  212.3 422.3 %all-gather.22.cloned.1.call-start = ((), (), s32[]{:S(2)}) async-start(), calls=%async_computation.11 | async-start | bytes 22560768 | tf_op jit(solution)/shard_map/all_gather | solution.py:160
  212.8 436.5 %all-gather.24.cloned.1.call-start = ((), (), s32[]{:S(2)}) async-start(), calls=%async_computation.12 | async-start | bytes 22560768 | tf_op jit(solution)/shard_map/all_gather | solution.py:161
  213.6 496.4 %reduce-scatter.11.cloned.1.call-start = ((), (), s32[]{:S(2)}) async-start(), calls=%async_computation.13 | async-start | bytes 2654208 | tf_op jit(solution)/shard_map/reduce_scatter | solution.py:216
  213.7 20.1 collective-permute-start
  214.0 29.4 %collective-permute-start.1 = (bf16[144,4608]{1,0:T(8,128)(2,1)S(1)}, bf16[144,4608]{1,0:T(8,128)(2,1)S(1)}, u32[]{:S(2)}, u32[]{:S(2)}) collective-permute-start(bf16[144,4608]{1,0:T(8,128)(2,1)S(1)} %copy-done.5), channel_id=1, source_target_pairs={{0,30},{2,0},{4,2},{6,4},{8,6},{10,8},{12,10},{14,12},{16,14},{18,... | collective-permute-start | bytes 3981320 | tf_op jit(solution)/shard_map/ppermute | solution.py:35
  233.7 74.6 %copy-start.26 = (bf16[144,4608]{1,0:T(8,128)(2,1)}, bf16[144,4608]{1,0:T(8,128)(2,1)S(1)}, u32[]{:S(2)}) copy-start(bf16[144,4608]{1,0:T(8,128)(2,1)S(1)} %collective-permute-done) | copy-start | bytes 3981316
  233.7 23.0 collective-permute-start.2
  244.4 63.9 %collective-permute-start.3 = (bf16[144,4608]{1,0:T(8,128)(2,1)S(1)}, bf16[144,4608]{1,0:T(8,128)(2,1)}, u32[]{:S(2)}, u32[]{:S(2)}) collective-permute-start(bf16[144,4608]{1,0:T(8,128)(2,1)S(1)} %collective-permute-done.1), channel_id=1, source_target_pairs={{0,30},{2,0},{4,2},{6,4},{8,6},{10,8},{12,10},{14,12},{16,14},{18,... | collective-permute-start | bytes 3981320 | tf_op jit(solution)/shard_map/ppermute | solution.py:35
  256.7 68.8 %collective-permute-start.4 = (bf16[144,4608]{1,0:T(8,128)(2,1)}, bf16[144,4608]{1,0:T(8,128)(2,1)}, u32[]{:S(2)}, u32[]{:S(2)}) collective-permute-start(bf16[144,4608]{1,0:T(8,128)(2,1)} %collective-permute-done.2), channel_id=1, source_target_pairs={{0,2},{2,4},{4,6},{6,8},{8,10},{10,12},{12,14},{14,16},{16,18},{18... | collective-permute-start | bytes 3981320 | tf_op jit(solution)/shard_map/ppermute | solution.py:27
  308.3 71.0 %collective-permute-start.5 = (bf16[144,4608]{1,0:T(8,128)(2,1)}, bf16[144,4608]{1,0:T(8,128)(2,1)}, u32[]{:S(2)}, u32[]{:S(2)}) collective-permute-start(bf16[144,4608]{1,0:T(8,128)(2,1)} %collective-permute-done.3), channel_id=1, source_target_pairs={{0,30},{2,0},{4,2},{6,4},{8,6},{10,8},{12,10},{14,12},{16,14},{18,... | collective-permute-start | bytes 3981320 | tf_op jit(solution)/shard_map/ppermute | solution.py:35
  325.5 70.1 %collective-permute-start.6 = (bf16[144,4608]{1,0:T(8,128)(2,1)}, bf16[144,4608]{1,0:T(8,128)(2,1)}, u32[]{:S(2)}, u32[]{:S(2)}) collective-permute-start(bf16[144,4608]{1,0:T(8,128)(2,1)} %collective-permute-done.4), channel_id=1, source_target_pairs={{0,2},{2,4},{4,6},{6,8},{8,10},{10,12},{12,14},{14,16},{16,18},{18... | collective-permute-start | bytes 3981320 | tf_op jit(solution)/shard_map/ppermute | solution.py:27
  376.7 236.9 %copy-start.37 = (f32[2304]{0:T(1024)}, f32[2304]{0:T(1024)S(1)}, u32[]{:S(2)}) copy-start(f32[2304]{0:T(1024)S(1)} %convert_element_type.111) | copy-start | bytes 27652
  379.4 60.9 %collective-permute-start.7 = (bf16[144,4608]{1,0:T(8,128)(2,1)}, bf16[144,4608]{1,0:T(8,128)(2,1)S(1)}, u32[]{:S(2)}, u32[]{:S(2)}) collective-permute-start(bf16[144,4608]{1,0:T(8,128)(2,1)} %collective-permute-done.5), channel_id=1, source_target_pairs={{0,30},{2,0},{4,2},{6,4},{8,6},{10,8},{12,10},{14,12},{16,14},{18,... | collective-permute-start | bytes 3981320 | tf_op jit(solution)/shard_map/ppermute | solution.py:35
  395.5 47.2 %collective-permute-start.8 = (bf16[144,4608]{1,0:T(8,128)(2,1)}, bf16[144,4608]{1,0:T(8,128)(2,1)S(1)}, u32[]{:S(2)}, u32[]{:S(2)}) collective-permute-start(bf16[144,4608]{1,0:T(8,128)(2,1)} %collective-permute-done.6), channel_id=1, source_target_pairs={{0,2},{2,4},{4,6},{6,8},{8,10},{10,12},{12,14},{14,16},{16,18},{18... | collective-permute-start | bytes 3981320 | tf_op jit(solution)/shard_map/ppermute | solution.py:27
  440.2 53.1 %collective-permute-start.9 = (bf16[144,4608]{1,0:T(8,128)(2,1)S(1)}, bf16[144,4608]{1,0:T(8,128)(2,1)S(1)}, u32[]{:S(2)}, u32[]{:S(2)}) collective-permute-start(bf16[144,4608]{1,0:T(8,128)(2,1)S(1)} %collective-permute-done.7), channel_id=1, source_target_pairs={{0,30},{2,0},{4,2},{6,4},{8,6},{10,8},{12,10},{14,12},{16,14},{18,... | collective-permute-start | bytes 3981320 | tf_op jit(solution)/shard_map/ppermute | solution.py:35
  442.7 61.9 %collective-permute-start.10 = (bf16[144,4608]{1,0:T(8,128)(2,1)S(1)}, bf16[144,4608]{1,0:T(8,128)(2,1)S(1)}, u32[]{:S(2)}, u32[]{:S(2)}) collective-permute-start(bf16[144,4608]{1,0:T(8,128)(2,1)S(1)} %collective-permute-done.8), channel_id=1, source_target_pairs={{0,2},{2,4},{4,6},{6,8},{8,10},{10,12},{12,14},{14,16},{16,18},{18... | collective-permute-start | bytes 3981320 | tf_op jit(solution)/shard_map/ppermute | solution.py:27
  493.3 57.2 %collective-permute-start.11 = (bf16[144,4608]{1,0:T(8,128)(2,1)S(1)}, bf16[144,4608]{1,0:T(8,128)(2,1)S(1)}, u32[]{:S(2)}, u32[]{:S(2)}) collective-permute-start(bf16[144,4608]{1,0:T(8,128)(2,1)S(1)} %collective-permute-done.9), channel_id=1, source_target_pairs={{0,30},{2,0},{4,2},{6,4},{8,6},{10,8},{12,10},{14,12},{16,14},{18,... | collective-permute-start | bytes 3981320 | tf_op jit(solution)/shard_map/ppermute | solution.py:35
  504.6 47.2 %collective-permute-start.12 = (bf16[144,4608]{1,0:T(8,128)(2,1)S(1)}, bf16[144,4608]{1,0:T(8,128)(2,1)S(1)}, u32[]{:S(2)}, u32[]{:S(2)}) collective-permute-start(bf16[144,4608]{1,0:T(8,128)(2,1)S(1)} %collective-permute-done.10), channel_id=1, source_target_pairs={{0,2},{2,4},{4,6},{6,8},{8,10},{10,12},{12,14},{14,16},{16,18},{18... | collective-permute-start | bytes 3981320 | tf_op jit(solution)/shard_map/ppermute | solution.py:27
  550.5 45.8 %collective-permute-start.13 = (bf16[144,4608]{1,0:T(8,128)(2,1)S(1)}, bf16[144,4608]{1,0:T(8,128)(2,1)S(1)}, u32[]{:S(2)}, u32[]{:S(2)}) collective-permute-start(bf16[144,4608]{1,0:T(8,128)(2,1)S(1)} %collective-permute-done.11), channel_id=1, source_target_pairs={{0,30},{2,0},{4,2},{6,4},{8,6},{10,8},{12,10},{14,12},{16,14},{18,... | collective-permute-start | bytes 3981320 | tf_op jit(solution)/shard_map/ppermute | solution.py:35
  551.8 57.7 %collective-permute-start.14 = (bf16[144,4608]{1,0:T(8,128)(2,1)S(1)}, bf16[144,4608]{1,0:T(8,128)(2,1)S(1)}, u32[]{:S(2)}, u32[]{:S(2)}) collective-permute-start(bf16[144,4608]{1,0:T(8,128)(2,1)S(1)} %collective-permute-done.12), channel_id=1, source_target_pairs={{0,2},{2,4},{4,6},{6,8},{8,10},{10,12},{12,14},{14,16},{16,18},{18... | collective-permute-start | bytes 3981320 | tf_op jit(solution)/shard_map/ppermute | solution.py:27
  649.3 62.1 %copy-start.8 = (bf16[96,2304]{1,0:T(8,128)(2,1)S(1)}, bf16[96,2304]{1,0:T(8,128)(2,1)}, u32[]{:S(2)}) copy-start(bf16[96,2304]{1,0:T(8,128)(2,1)} %param.27) | copy-start | bytes 1327108
  662.0 163.9 %all-gather.26.cloned.1.call-start = ((), (), s32[]{:S(2)}) async-start(), calls=%async_computation.14 | async-start | bytes 22560768 | tf_op jit(solution)/shard_map/all_gather | solution.py:245
  715.7 221.6 %all-gather.28.cloned.1.call-start = ((), (), s32[]{:S(2)}) async-start(), calls=%async_computation.15 | async-start | bytes 22560768 | tf_op jit(solution)/shard_map/all_gather | solution.py:243
  716.3 332.7 %all-gather.30.cloned.1.call-start = ((), (), s32[]{:S(2)}) async-start(), calls=%async_computation.16 | async-start | bytes 22560768 | tf_op jit(solution)/shard_map/all_gather | solution.py:244
  717.0 373.5 %reduce-scatter.13.cloned.1.call-start = ((), (), s32[]{:S(2)}) async-start(), calls=%async_computation.17 | async-start | bytes 2654208 | tf_op jit(solution)/shard_map/reduce_scatter | solution.py:268
  729.7 110.4 %copy-start.6 = (bf16[192,2304]{1,0:T(8,128)(2,1)}, bf16[192,2304]{1,0:T(8,128)(2,1)S(1)}, u32[]{:S(2)}) copy-start(bf16[192,2304]{1,0:T(8,128)(2,1)S(1)} %all_gather.75) | copy-start | bytes 2654212
  1062.1 83.9 %all-gather.32.cloned.1.call-start = ((), (), s32[]{:S(2)}) async-start(), calls=%async_computation.18 | async-start | bytes 5013504 | tf_op jit(solution)/shard_map/all_gather | solution.py:242
  1062.9 137.0 %all-gather.34.cloned.1.call-start = ((), (), s32[]{:S(2)}) async-start(), calls=%async_computation.19 | async-start | bytes 5013504 | tf_op jit(solution)/shard_map/all_gather | solution.py:239
  1063.4 179.4 %all-gather.36.cloned.1.call-start = ((), (), s32[]{:S(2)}) async-start(), calls=%async_computation.20 | async-start | bytes 2506752 | tf_op jit(solution)/shard_map/all_gather | solution.py:240
  1064.0 222.0 %all-gather.38.cloned.1.call-start = ((), (), s32[]{:S(2)}) async-start(), calls=%async_computation.21 | async-start | bytes 2506752 | tf_op jit(solution)/shard_map/all_gather | solution.py:241
  1064.6 419.1 %reduce-scatter.15.cloned.1.call-start = ((), (), s32[]{:S(2)}) async-start(), calls=%async_computation.22 | async-start | bytes 1327104 | tf_op jit(solution)/shard_map/reduce_scatter | solution.py:339
  1289.6 318.4 %reduce-scatter.19.cloned.1.call-start = ((), (), s32[]{:S(2)}) async-start(), calls=%async_computation.24 | async-start | bytes 30081024
  1336.3 1452.6 %reduce-scatter.17.cloned.1.call-start = ((), (), s32[]{:S(2)}) async-start(), calls=%async_computation.23 | async-start | bytes 135364608 | tf_op jit(solution)/shard_map/reduce_scatter | solution.py:258
  1483.6 45.5 %copy-start.4 = (f32[96,2304]{1,0:T(8,128)S(1)}, f32[96,2304]{1,0:T(8,128)}, u32[]{:S(2)}) copy-start(f32[96,2304]{1,0:T(8,128)} %copy-done.3) | copy-start | bytes 2654212
  (38 other events, 548.9 us)
Sparse Core Ops, SparseCore 0:
  10.3 45.2 all-gather.15
  57.8 41.0 all-gather.13
  101.3 51.8 all-gather.17
  155.3 51.6 all-gather.19
  212.4 26.8 reduce-scatter.8
  240.7 208.0 all-gather.21
  450.4 184.2 all-gather.23
  662.1 47.8 reduce-scatter.10
  715.8 110.0 all-gather.25
  827.3 109.9 all-gather.27
  938.9 109.9 all-gather.29
  1062.2 28.2 reduce-scatter.12
  1092.8 53.1 all-gather.31
  1148.1 51.6 all-gather.33
  1202.0 40.8 all-gather.35
  1245.0 41.0 all-gather.37
  1289.7 17.3 reduce-scatter.14
  1336.4 271.5 reduce-scatter.18
  1612.3 1176.6 reduce-scatter.16
